TPU v7x, 32 devices: a whole 2x2x4 slice. The times are simulated.
32 devices in a mesh: dp: 8 (over y, x, core), fsdp: 4 (over z).
Axes of the slice: x: 2, y: 2, z: 4, core: 2. Of those that a mesh axis runs over, the one named last changes fastest.
Arguments:
- inputs: bfloat16 [32768, 768], P(('dp', 'fsdp')), may hold values from -6 to 6
- segment_ids: int32 [32, 1024], P(('dp', 'fsdp')), may hold values from 0 to 7, never falling along the last dimension, each value on 1 to 256 neighbouring positions
- cotangent: bfloat16 [32768, 768], P(('dp', 'fsdp')), may hold values from -6 to 6
- ln1_gain: float32 [768], P(('dp', 'fsdp')), may hold values from 0.5 to 1.5
- ln1_bias: float32 [768], P(('dp', 'fsdp')), may hold values from -1.75 to 1.75
- w_query: float32 [768, 768], P(('dp', 'fsdp')), may hold values from -0.3125 to 0.3125
- b_query: float32 [768], P(('dp', 'fsdp')), may hold values from -1.75 to 1.75
- w_key: float32 [768, 768], P(('dp', 'fsdp')), may hold values from -0.3125 to 0.3125
- w_value: float32 [768, 768], P(('dp', 'fsdp')), may hold values from -0.21875 to 0.21875
- b_value: float32 [768], P(('dp', 'fsdp')), may hold values from -1.75 to 1.75
- w_out: float32 [768, 768], P(('dp', 'fsdp')), may hold values from -0.875 to 0.875
- b_out: float32 [768], P(('dp', 'fsdp')), may hold values from -1.75 to 1.75
- ln2_gain: float32 [768], P(('dp', 'fsdp')), may hold values from 0.5 to 1.5
- ln2_bias: float32 [768], P(('dp', 'fsdp')), may hold values from -1.75 to 1.75
- w_up: float32 [768, 3072], P(('dp', 'fsdp')), may hold values from -0.21875 to 0.21875
- b_up: float32 [3072], P(('dp', 'fsdp')), may hold values from -1.75 to 1.75
- w_down: float32 [3072, 768], P(('dp', 'fsdp')), may hold values from -0.109375 to 0.109375
- b_down: float32 [768], P(('dp', 'fsdp')), may hold values from -1.75 to 1.75
Outputs:
- block_output: bfloat16 [32768, 768], P(('dp', 'fsdp'))
- input_grad: float32 [32768, 768], P(('dp', 'fsdp'))
- grad_ln1_gain: float32 [768], P(('dp', 'fsdp'))
- grad_ln1_bias: float32 [768], P(('dp', 'fsdp'))
- grad_w_query: float32 [768, 768], P(('dp', 'fsdp'))
- grad_b_query: float32 [768], P(('dp', 'fsdp'))
- grad_w_key: float32 [768, 768], P(('dp', 'fsdp'))
- grad_w_value: float32 [768, 768], P(('dp', 'fsdp'))
- grad_b_value: float32 [768], P(('dp', 'fsdp'))
- grad_w_out: float32 [768, 768], P(('dp', 'fsdp'))
- grad_b_out: float32 [768], P(('dp', 'fsdp'))
- grad_ln2_gain: float32 [768], P(('dp', 'fsdp'))
- grad_ln2_bias: float32 [768], P(('dp', 'fsdp'))
- grad_w_up: float32 [768, 3072], P(('dp', 'fsdp'))
- grad_b_up: float32 [3072], P(('dp', 'fsdp'))
- grad_w_down: float32 [3072, 768], P(('dp', 'fsdp'))
- grad_b_down: float32 [768], P(('dp', 'fsdp'))
Inputs may be any that keep to these rules, and one draw needn't show every extreme that they name: `segment_ids`: each row of 1024 tokens holds 8 documents numbered 0 to 7 in order, never falling, each 1 to 256 tokens long, one of exactly 256.
All inputs are finite; a program needn't handle non-finite values.
Results may differ from a plain program's by a relative error of at most 0.013.
The roundings to bfloat16 on the way count: a program that leaves them out, or rounds other values in their place, can miss the bound.
Values may be sent and summed in bfloat16 or wider, within the bound.
A program may use at most 320 MiB of HBM per device.

v0:
```python
import jax
import jax.numpy as jnp
from jax import lax
from jax.sharding import PartitionSpec as P

HEAD = 64


NORM_EPSILON = 1e-12
MASK_VALUE = -1e30


def layer_norm(vector_rows, gain_row, bias_row):
    centre = vector_rows - jnp.mean(vector_rows, axis=-1, keepdims=True)
    spread = jnp.mean(centre * centre, axis=-1, keepdims=True)
    return centre * lax.rsqrt(spread + NORM_EPSILON) * gain_row + bias_row


def exact_gelu(up_values):
    return jax.nn.gelu(up_values, approximate=False)


def matmul(left_arg, right_arg):
    return jnp.dot(left_arg, right_arg, preferred_element_type=jnp.float32)


def matmul_left_t(left_arg, right_arg):
    return lax.dot_general(
        left_arg, right_arg, (((0,), (0,)), ((), ())), preferred_element_type=jnp.float32
    )


def matmul_right_t(left_arg, right_arg):
    return lax.dot_general(
        left_arg, right_arg, (((1,), (1,)), ((), ())), preferred_element_type=jnp.float32
    )


def to_low(array_in):
    return array_in.astype(jnp.bfloat16)


def widen(array_in):
    return array_in.astype(jnp.float32)


def block_scores(query_block, key_rows, seg_query, seg_keys):
    scores = (
        jnp.einsum("qhe,khe->hqk", query_block, key_rows, preferred_element_type=jnp.float32)
        * 0.125
    )
    same_doc = seg_query[:, None] == seg_keys[None, :]
    return jnp.where(same_doc[None, :, :], scores, MASK_VALUE)


def attend_forward(queries, key_rows, values, segments):
    length = queries.shape[0]
    block_rows = min(512, length)
    pieces = []
    totals = []
    for offset in range(0, length, block_rows):
        scores = block_scores(
            queries[offset : offset + block_rows],
            key_rows,
            segments[offset : offset + block_rows],
            segments,
        )
        row_max = jnp.max(scores, axis=-1, keepdims=True)
        raised = jnp.exp(scores - row_max)
        row_sum = jnp.sum(raised, axis=-1, keepdims=True)
        prob_low = (raised / row_sum).astype(jnp.bfloat16)
        pieces.append(
            jnp.einsum("hqk,khe->qhe", prob_low, values, preferred_element_type=jnp.float32)
        )
        totals.append(row_max + jnp.log(row_sum))
    return (jnp.concatenate(pieces, 0), jnp.concatenate(totals, 1))


def attend_backward(queries, key_rows, values, segments, log_totals, grad_mixed):
    length = queries.shape[0]
    block_rows = min(512, length)
    grad_query_parts = []
    grad_keys = jnp.zeros(key_rows.shape, jnp.float32)
    grad_values = jnp.zeros(values.shape, jnp.float32)
    for offset in range(0, length, block_rows):
        query_block = queries[offset : offset + block_rows]
        grad_block = grad_mixed[offset : offset + block_rows]
        scores = block_scores(
            query_block, key_rows, segments[offset : offset + block_rows], segments
        )
        prob_rows = jnp.exp(scores - log_totals[:, offset : offset + block_rows, :])
        prob_low = prob_rows.astype(jnp.bfloat16)
        grad_prob = jnp.einsum(
            "qhe,khe->hqk", grad_block, values, preferred_element_type=jnp.float32
        )
        centre_term = jnp.sum(prob_rows * grad_prob, axis=-1, keepdims=True)
        grad_scores = (prob_rows * (grad_prob - centre_term)).astype(jnp.bfloat16)
        grad_query_parts.append(
            jnp.einsum("hqk,khe->qhe", grad_scores, key_rows, preferred_element_type=jnp.float32)
            * 0.125
        )
        grad_keys = (
            grad_keys
            + jnp.einsum(
                "hqk,qhe->khe", grad_scores, query_block, preferred_element_type=jnp.float32
            )
            * 0.125
        )
        grad_values = grad_values + jnp.einsum(
            "hqk,qhe->khe", prob_low, grad_block, preferred_element_type=jnp.float32
        )
    return (jnp.concatenate(grad_query_parts, 0), grad_keys, grad_values)


def forward_pass(weights, inputs, segment_ids):
    (
        ln1_gain,
        ln1_bias,
        w_query,
        b_query,
        w_key,
        w_value,
        b_value,
        w_out,
        b_out,
        ln2_gain,
        ln2_bias,
        w_up,
        b_up,
        w_down,
        b_down,
    ) = weights
    token_count = inputs.shape[0]
    head_count = w_query.shape[1] // HEAD
    tokens_f = widen(inputs)
    normed_one = to_low(layer_norm(tokens_f, widen(ln1_gain), widen(ln1_bias)))
    queries = to_low(matmul(normed_one, w_query) + widen(b_query)).reshape(
        token_count, head_count, HEAD
    )
    key_rows = to_low(matmul(normed_one, w_key)).reshape(token_count, head_count, HEAD)
    values = to_low(matmul(normed_one, w_value) + widen(b_value)).reshape(
        token_count, head_count, HEAD
    )
    attended, totals = attend_forward(queries, key_rows, values, segment_ids[0])
    total_parts = [totals]
    mixed = to_low(attended.reshape(token_count, head_count * HEAD))
    hidden_one = tokens_f + matmul(mixed, w_out) + widen(b_out)
    normed_two = to_low(layer_norm(hidden_one, widen(ln2_gain), widen(ln2_bias)))
    up_rows = matmul(normed_two, w_up) + widen(b_up)
    activated = to_low(exact_gelu(up_rows))
    result = hidden_one + matmul(activated, w_down) + widen(b_down)
    return (
        tokens_f,
        normed_one,
        queries,
        key_rows,
        values,
        total_parts,
        mixed,
        hidden_one,
        normed_two,
        up_rows,
        activated,
        result,
    )


def backward_ffn(weights, kept_values, cotangent):
    (
        ln1_gain,
        ln1_bias,
        w_query,
        b_query,
        w_key,
        w_value,
        b_value,
        w_out,
        b_out,
        ln2_gain,
        ln2_bias,
        w_up,
        b_up,
        w_down,
        b_down,
    ) = weights
    (
        tokens_f,
        normed_one,
        queries,
        key_rows,
        values,
        total_parts,
        mixed,
        hidden_one,
        normed_two,
        up_rows,
        activated,
        result,
    ) = kept_values
    cotangent_f = widen(cotangent)
    grad_w_down = matmul_left_t(activated, cotangent)
    grad_b_down = jnp.sum(cotangent_f, axis=0)
    grad_activated = matmul_right_t(cotangent, w_down)
    gelu_pullback = jax.vjp(exact_gelu, up_rows)[1]
    grad_up = to_low(gelu_pullback(grad_activated)[0])
    grad_w_up = matmul_left_t(normed_two, grad_up)
    grad_b_up = jnp.sum(widen(grad_up), axis=0)
    grad_normed_two = matmul_right_t(grad_up, w_up)
    norm_pullback = jax.vjp(layer_norm, hidden_one, widen(ln2_gain), widen(ln2_bias))[1]
    grad_hidden_norm, grad_ln2_gain, grad_ln2_bias = norm_pullback(grad_normed_two)
    grad_hidden = cotangent_f + grad_hidden_norm
    return (
        (grad_ln2_gain, grad_ln2_bias, grad_w_up, grad_b_up, grad_w_down, grad_b_down),
        grad_hidden,
    )


def backward_attention(weights, kept_values, segment_ids, grad_hidden):
    (
        ln1_gain,
        ln1_bias,
        w_query,
        b_query,
        w_key,
        w_value,
        b_value,
        w_out,
        b_out,
        ln2_gain,
        ln2_bias,
        w_up,
        b_up,
        w_down,
        b_down,
    ) = weights
    (
        tokens_f,
        normed_one,
        queries,
        key_rows,
        values,
        total_parts,
        mixed,
        hidden_one,
        normed_two,
        up_rows,
        activated,
        result,
    ) = kept_values
    token_count = queries.shape[0]
    head_count = queries.shape[1]
    grad_branch = to_low(grad_hidden)
    grad_w_out = matmul_left_t(mixed, grad_branch)
    grad_b_out = jnp.sum(widen(grad_branch), axis=0)
    grad_mixed = to_low(matmul_right_t(grad_branch, w_out)).reshape(token_count, head_count, HEAD)
    grad_q_part, grad_k_part, grad_v_part = attend_backward(
        queries, key_rows, values, segment_ids[0], total_parts[0], grad_mixed
    )
    grad_queries = to_low(grad_q_part.reshape(token_count, head_count * HEAD))
    grad_keys = to_low(grad_k_part.reshape(token_count, head_count * HEAD))
    grad_values = to_low(grad_v_part.reshape(token_count, head_count * HEAD))
    grad_w_query = matmul_left_t(normed_one, grad_queries)
    grad_b_query = jnp.sum(widen(grad_queries), axis=0)
    grad_w_key = matmul_left_t(normed_one, grad_keys)
    grad_w_value = matmul_left_t(normed_one, grad_values)
    grad_b_value = jnp.sum(widen(grad_values), axis=0)
    grad_normed_one = (
        matmul_right_t(grad_queries, w_query)
        + matmul_right_t(grad_keys, w_key)
        + matmul_right_t(grad_values, w_value)
    )
    norm_pullback = jax.vjp(layer_norm, tokens_f, widen(ln1_gain), widen(ln1_bias))[1]
    grad_inputs_norm, grad_ln1_gain, grad_ln1_bias = norm_pullback(grad_normed_one)
    input_grad = grad_hidden + grad_inputs_norm
    return (
        (
            grad_ln1_gain,
            grad_ln1_bias,
            grad_w_query,
            grad_b_query,
            grad_w_key,
            grad_w_value,
            grad_b_value,
            grad_w_out,
            grad_b_out,
        ),
        input_grad,
    )


def shards(
    inputs,
    segment_ids,
    cotangent,
    ln1_gain,
    ln1_bias,
    w_query,
    b_query,
    w_key,
    w_value,
    b_value,
    w_out,
    b_out,
    ln2_gain,
    ln2_bias,
    w_up,
    b_up,
    w_down,
    b_down,
):
    gathered = (
        lax.all_gather(to_low(ln1_gain), ("dp", "fsdp"), axis=0, tiled=True),
        lax.all_gather(to_low(ln1_bias), ("dp", "fsdp"), axis=0, tiled=True),
        lax.all_gather(to_low(w_query), ("dp", "fsdp"), axis=0, tiled=True),
        lax.all_gather(to_low(b_query), ("dp", "fsdp"), axis=0, tiled=True),
        lax.all_gather(to_low(w_key), ("dp", "fsdp"), axis=0, tiled=True),
        lax.all_gather(to_low(w_value), ("dp", "fsdp"), axis=0, tiled=True),
        lax.all_gather(to_low(b_value), ("dp", "fsdp"), axis=0, tiled=True),
        lax.all_gather(to_low(w_out), ("dp", "fsdp"), axis=0, tiled=True),
        lax.all_gather(to_low(b_out), ("dp", "fsdp"), axis=0, tiled=True),
        lax.all_gather(to_low(ln2_gain), ("dp", "fsdp"), axis=0, tiled=True),
        lax.all_gather(to_low(ln2_bias), ("dp", "fsdp"), axis=0, tiled=True),
        lax.all_gather(to_low(w_up), ("dp", "fsdp"), axis=0, tiled=True),
        lax.all_gather(to_low(b_up), ("dp", "fsdp"), axis=0, tiled=True),
        lax.all_gather(to_low(w_down), ("dp", "fsdp"), axis=0, tiled=True),
        lax.all_gather(to_low(b_down), ("dp", "fsdp"), axis=0, tiled=True),
    )
    first_pass = forward_pass(gathered, inputs, segment_ids)
    block_output = first_pass[11].astype(jnp.bfloat16)
    back_weights = (
        lax.all_gather(to_low(ln1_gain), ("dp", "fsdp"), axis=0, tiled=True),
        lax.all_gather(to_low(ln1_bias), ("dp", "fsdp"), axis=0, tiled=True),
        lax.all_gather(to_low(w_query), ("dp", "fsdp"), axis=0, tiled=True),
        lax.all_gather(to_low(b_query), ("dp", "fsdp"), axis=0, tiled=True),
        lax.all_gather(to_low(w_key), ("dp", "fsdp"), axis=0, tiled=True),
        lax.all_gather(to_low(w_value), ("dp", "fsdp"), axis=0, tiled=True),
        lax.all_gather(to_low(b_value), ("dp", "fsdp"), axis=0, tiled=True),
        lax.all_gather(to_low(w_out), ("dp", "fsdp"), axis=0, tiled=True),
        lax.all_gather(to_low(b_out), ("dp", "fsdp"), axis=0, tiled=True),
        lax.all_gather(to_low(ln2_gain), ("dp", "fsdp"), axis=0, tiled=True),
        lax.all_gather(to_low(ln2_bias), ("dp", "fsdp"), axis=0, tiled=True),
        lax.all_gather(to_low(w_up), ("dp", "fsdp"), axis=0, tiled=True),
        lax.all_gather(to_low(b_up), ("dp", "fsdp"), axis=0, tiled=True),
        lax.all_gather(to_low(w_down), ("dp", "fsdp"), axis=0, tiled=True),
        lax.all_gather(to_low(b_down), ("dp", "fsdp"), axis=0, tiled=True),
    )
    kept_values = forward_pass(back_weights, inputs, segment_ids)
    ffn_terms, grad_hidden = backward_ffn(back_weights, kept_values, cotangent)
    term_ln2_gain, term_ln2_bias, term_w_up, term_b_up, term_w_down, term_b_down = ffn_terms
    attn_terms, input_grad = backward_attention(back_weights, kept_values, segment_ids, grad_hidden)
    (
        term_ln1_gain,
        term_ln1_bias,
        term_w_query,
        term_b_query,
        term_w_key,
        term_w_value,
        term_b_value,
        term_w_out,
        term_b_out,
    ) = attn_terms
    all_shards = (
        lax.psum_scatter(term_ln1_gain, ("dp", "fsdp"), scatter_dimension=0, tiled=True),
        lax.psum_scatter(term_ln1_bias, ("dp", "fsdp"), scatter_dimension=0, tiled=True),
        lax.psum_scatter(term_w_query, ("dp", "fsdp"), scatter_dimension=0, tiled=True),
        lax.psum_scatter(term_b_query, ("dp", "fsdp"), scatter_dimension=0, tiled=True),
        lax.psum_scatter(term_w_key, ("dp", "fsdp"), scatter_dimension=0, tiled=True),
        lax.psum_scatter(term_w_value, ("dp", "fsdp"), scatter_dimension=0, tiled=True),
        lax.psum_scatter(term_b_value, ("dp", "fsdp"), scatter_dimension=0, tiled=True),
        lax.psum_scatter(term_w_out, ("dp", "fsdp"), scatter_dimension=0, tiled=True),
        lax.psum_scatter(term_b_out, ("dp", "fsdp"), scatter_dimension=0, tiled=True),
        lax.psum_scatter(term_ln2_gain, ("dp", "fsdp"), scatter_dimension=0, tiled=True),
        lax.psum_scatter(term_ln2_bias, ("dp", "fsdp"), scatter_dimension=0, tiled=True),
        lax.psum_scatter(term_w_up, ("dp", "fsdp"), scatter_dimension=0, tiled=True),
        lax.psum_scatter(term_b_up, ("dp", "fsdp"), scatter_dimension=0, tiled=True),
        lax.psum_scatter(term_w_down, ("dp", "fsdp"), scatter_dimension=0, tiled=True),
        lax.psum_scatter(term_b_down, ("dp", "fsdp"), scatter_dimension=0, tiled=True),
    )
    return (
        block_output,
        input_grad,
        all_shards[0],
        all_shards[1],
        all_shards[2],
        all_shards[3],
        all_shards[4],
        all_shards[5],
        all_shards[6],
        all_shards[7],
        all_shards[8],
        all_shards[9],
        all_shards[10],
        all_shards[11],
        all_shards[12],
        all_shards[13],
        all_shards[14],
    )


def solution(mesh):
    placed = (
        P(("dp", "fsdp"), None),
        P(("dp", "fsdp"), None),
        P(("dp", "fsdp"), None),
        P(("dp", "fsdp")),
        P(("dp", "fsdp")),
        P(("dp", "fsdp"), None),
        P(("dp", "fsdp")),
        P(("dp", "fsdp"), None),
        P(("dp", "fsdp"), None),
        P(("dp", "fsdp")),
        P(("dp", "fsdp"), None),
        P(("dp", "fsdp")),
        P(("dp", "fsdp")),
        P(("dp", "fsdp")),
        P(("dp", "fsdp"), None),
        P(("dp", "fsdp")),
        P(("dp", "fsdp"), None),
        P(("dp", "fsdp")),
    )
    return jax.shard_map(
        shards,
        mesh=mesh,
        in_specs=placed,
        out_specs=(
            P(("dp", "fsdp"), None),
            P(("dp", "fsdp"), None),
            P(("dp", "fsdp")),
            P(("dp", "fsdp")),
            P(("dp", "fsdp"), None),
            P(("dp", "fsdp")),
            P(("dp", "fsdp"), None),
            P(("dp", "fsdp"), None),
            P(("dp", "fsdp")),
            P(("dp", "fsdp"), None),
            P(("dp", "fsdp")),
            P(("dp", "fsdp")),
            P(("dp", "fsdp")),
            P(("dp", "fsdp"), None),
            P(("dp", "fsdp")),
            P(("dp", "fsdp"), None),
            P(("dp", "fsdp")),
        ),
        check_vma=False,
    )
```

profile of v0, /device:TPU:0, one launch (start us, length us, event | category | flops | bytes accessed | tf_op | source)
XLA Modules:
  0.0 1116.2 jit_solution(14627392873056501546)
XLA Ops:
  25.5 43.3 %all-reduce.19 = (bf16[768]{0:T(1024)(128)(2,1)S(1)}, bf16[768]{0:T(1024)(128)(2,1)S(1)}, bf16[768]{0:T(1024)(128)(2,1)S(1)}, bf16[768]{0:T(1024)(128)(2,1)S(1)}...) all-reduce(bf16[768]{0:T(1024)(128)(2,1)S(1)} %dynamic-update-slice, ...), channel_id=1, replica_groups=mesh['dp'=8,'fsdp'=4] {'dp','fsdp'}, use_global_device_ids=true, to_apply=%add.2 | all-reduce | flops 9216 | bytes 36864
  80.6 44.0 %all-gather.11.cloned.1.call-done = bf16[768,768]{1,0:T(8,128)(2,1)} async-done(((bf16[24,768]{1,0:T(8,128)(2,1)}), bf16[768,768]{1,0:T(8,128)(2,1)}) %all-gather.11.cloned.1.call-update) | async-done | bytes 1179664 | tf_op jit(solution)/shard_map/all_gather | solution.py:316
  127.6 10.7 fusion.18
  138.3 11.8 %fusion = f32[12,512]{1,0:T(8,128)S(1)} fusion(f32[12,512]{1,0:T(8,128)S(1)} %get-tuple-element.95, f32[12,512,1024]{2,1,0:T(8,128)} %get-tuple-element.96, pred[512,1024]{1,0:T(8,128)(4,1)S(1)} %copy-done.13), kind=kLoop, calls=%fused_computation.12 | loop fusion | flops 25159680 | bytes 25739264 | tf_op jit(solution)/shard_map/reduce_sum | solution.py:70
  150.8 30.2 %all-gather.7.cloned.1.call-done = bf16[768,768]{1,0:T(8,128)(2,1)} async-done(((bf16[24,768]{1,0:T(8,128)(2,1)}), bf16[768,768]{1,0:T(8,128)(2,1)}) %all-gather.7.cloned.1.call-update) | async-done | bytes 1179664 | tf_op jit(solution)/shard_map/all_gather | solution.py:317
  184.0 13.6 %fusion.37 = bf16[512,12,64]{0,2,1:T(8,128)(2,1)} fusion(bf16[1024,12,64]{0,2,1:T(8,128)(2,1)S(1)} %bitcast.81, f32[12,512]{1,0:T(8,128)S(1)} %fusion, f32[12,512]{1,0:T(8,128)S(1)} %get-tuple-element.95, f32[12,512,1024]{2,1,0:T(8,128)} %get-tuple-element.96, pred[512,1024]{1,0:T(8,128)(4,1)S(1)} %copy-done.14), kind=kOutput, calls=%fused_computation.84 | convolution fusion | flops 837156864 | bytes 28098560 | tf_op jit(solution)/shard_map/hqk,khe->qhe/dot_general | solution.py:73
  197.6 10.7 fusion.19
  208.3 12.3 %fusion.1 = f32[12,512]{1,0:T(8,128)S(1)} fusion(f32[12,512]{1,0:T(8,128)S(1)} %get-tuple-element.93, f32[12,512,1024]{2,1,0:T(8,128)} %get-tuple-element.94, pred[512,1024]{1,0:T(8,128)(4,1)S(1)} %copy-done.16), kind=kLoop, calls=%fused_computation.13 | loop fusion | flops 25159680 | bytes 25739264 | tf_op jit(solution)/shard_map/reduce_sum | solution.py:70
  242.3 60.8 %all-gather.15.cloned.1.call-done = bf16[768,3072]{1,0:T(8,128)(2,1)} async-done(((bf16[24,3072]{1,0:T(8,128)(2,1)}), bf16[768,3072]{1,0:T(8,128)(2,1)}) %all-gather.15.cloned.1.call-update) | async-done | bytes 4718608 | tf_op jit(solution)/shard_map/all_gather | solution.py:323
  303.1 37.9 %multiply_convert_fusion.2 = (bf16[1024,3072]{1,0:T(8,128)(2,1)}, f32[1024,3072]{1,0:T(8,128)}, f32[1024,3072]{1,0:T(8,128)}) fusion(f32[3072]{0:T(1024)S(1)} %copy-done.57, bf16[768,3072]{1,0:T(8,128)(2,1)} %all-gather.15.cloned.1.call-done, f32[1024,768]{0,1:T(8,128)} %copy-done.7, f32[768]{0:T(1024)S(1)} %copy-done.60, f32[768]{0:T(1024)S(1)} %copy-done.50, ...), kind=kOutput, calls=%fused_computation.24 | convolution fusion | flops 5043388416 | bytes 39348224 | tf_op jit(solution)/shard_map/dot_general | solution.py:24
  341.0 27.2 %all-gather.17.cloned.1.call-done = bf16[3072,768]{1,0:T(8,128)(2,1)} async-done(((bf16[96,768]{1,0:T(8,128)(2,1)}), bf16[3072,768]{1,0:T(8,128)(2,1)}) %all-gather.17.cloned.1.call-update) | async-done | bytes 4718608 | tf_op jit(solution)/shard_map/all_gather | solution.py:325
  368.1 17.4 %convert_reduce_fusion = (f32[3072]{0:T(1024)}, bf16[1024,3072]{1,0:T(8,128)(2,1)}) fusion(f32[1024,3072]{1,0:T(8,128)} %get-tuple-element.82, bf16[1024,768]{1,0:T(8,128)(2,1)S(1)} %copy-done.27, bf16[3072,768]{1,0:T(8,128)(2,1)} %all-gather.17.cloned.1.call-done, f32[1024,3072]{1,0:T(8,128)} %get-tuple-element.99, f32[3072]{0:T(1024)S(1)} %copy-done.57), kind=kOutput, calls=%fused_computation.20 | convolution fusion | flops 4885312512 | bytes 37773312 | tf_op jit(solution)/shard_map/dot_general | solution.py:34
  385.5 10.7 fusion.69
  414.4 13.6 %fusion.5 = f32[12,64,1024]{2,1,0:T(8,128)} fusion(bf16[512,12,64]{0,2,1:T(8,128)(2,1)S(1)} %bitcast.87, f32[12,512]{1,0:T(8,128)S(1)} %copy-done.39, f32[12,512,1024]{2,1,0:T(8,128)} %get-tuple-element.94, pred[512,1024]{1,0:T(8,128)(4,1)S(1)} %copy-done.17), kind=kOutput, calls=%fused_computation.18 | convolution fusion | flops 830472192 | bytes 29646848 | tf_op jit(solution)/shard_map/hqk,qhe->khe/dot_general | solution.py:109
  428.0 17.9 %multiply_reduce_fusion.1 = (f32[12,512]{1,0:T(8,128)S(1)}, f32[12,512,1024]{2,1,0:T(8,128)}) fusion(f32[12,512]{1,0:T(8,128)S(1)} %copy-done.38, f32[12,512,1024]{2,1,0:T(8,128)} %get-tuple-element.96, pred[512,1024]{1,0:T(8,128)(4,1)S(1)} %copy-done.15, bf16[512,12,64]{0,2,1:T(8,128)(2,1)} %bitcast.89, bf16[1024,12,64]{0,2,1:T(8,128)(2,1)S(1)} %bitcast.83), kind=kOutput, calls=%fused_computation.4 | convolution fusion | flops 836757504 | bytes 53264384 | tf_op jit(solution)/shard_map/qhe,khe->hqk/dot_general | solution.py:93
  445.9 13.8 %convert_reduce_fusion.4 = (f32[12,64]{1,0:T(8,128)}, bf16[12,64,1024]{2,1,0:T(8,128)(2,1)S(1)}) fusion(f32[12,64,1024]{2,1,0:T(8,128)} %fusion.5, bf16[512,12,64]{0,2,1:T(8,128)(2,1)} %bitcast.90, f32[12,512]{1,0:T(8,128)S(1)} %copy-done.38, f32[12,512,1024]{2,1,0:T(8,128)} %get-tuple-element.96, pred[512,1024]{1,0:T(8,128)(4,1)S(1)} %copy-done.15), kind=kOutput, calls=%fused_computation.64 | convolution fusion | flops 833617152 | bytes 31222784 | tf_op jit(solution)/shard_map/hqk,qhe->khe/dot_general | solution.py:109
  463.9 21.9 %multiply_reduce_fusion = (f32[12,512]{1,0:T(8,128)S(1)}, f32[12,512,1024]{2,1,0:T(8,128)}) fusion(f32[12,512]{1,0:T(8,128)S(1)} %copy-done.39, f32[12,512,1024]{2,1,0:T(8,128)} %get-tuple-element.94, pred[512,1024]{1,0:T(8,128)(4,1)S(1)} %copy-done.17, bf16[512,12,64]{0,2,1:T(8,128)(2,1)S(1)} %bitcast.88, bf16[1024,12,64]{0,2,1:T(8,128)(2,1)S(1)} %bitcast.84), kind=kOutput, calls=%fused_computation.1 | convolution fusion | flops 836757504 | bytes 53264384 | tf_op jit(solution)/shard_map/qhe,khe->hqk/dot_general | solution.py:93
  485.9 42.1 %multiply_convert_fusion = (bf16[12,512,1024]{2,1,0:T(8,128)(2,1)}, bf16[12,512,1024]{2,1,0:T(8,128)(2,1)}) fusion(f32[12,512,1024]{2,1,0:T(8,128)} %get-tuple-element.101, f32[12,512]{1,0:T(8,128)S(1)} %get-tuple-element.100, f32[12,512]{1,0:T(8,128)S(1)} %copy-done.39, f32[12,512,1024]{2,1,0:T(8,128)} %get-tuple-element.94, ...), kind=kLoop, calls=%fused_computation | loop fusion | flops 75497472 | bytes 126976000 | tf_op jit(solution)/shard_map/convert_element_type | solution.py:97
  569.0 10.7 fusion.50
  617.1 39.9 %all-reduce.18 = (f32[768]{0:T(1024)S(1)}, f32[768]{0:T(1024)S(1)}, f32[768]{0:T(1024)S(1)}, f32[768]{0:T(1024)S(1)}, f32[768]{0:T(1024)S(1)}, /*index=5*/f32[76...) all-reduce(f32[768]{0:T(1024)S(1)} %get-tuple-element.53, ...), channel_id=2, replica_groups=mesh['dp'=8,'fsdp'=4] {'dp','fsdp'}, use_global_device_ids=true, to_apply=%region_15.16.clone | all-reduce | flops 9216 | bytes 73728
  665.8 55.5 %reduce-scatter.7.cloned.1.call-done = f32[24,768]{1,0:T(8,128)} async-done(((f32[768,768]{1,0:T(8,128)}), f32[24,768]{1,0:T(8,128)}) %reduce-scatter.7.cloned.1.call-update) | async-done | bytes 73744 | tf_op jit(solution)/shard_map/reduce_scatter | solution.py:365
  721.3 104.4 %reduce-scatter.9.cloned.1.call-done = f32[24,768]{1,0:T(8,128)} async-done(((f32[768,768]{1,0:T(8,128)}), f32[24,768]{1,0:T(8,128)}) %reduce-scatter.9.cloned.1.call-update) | async-done | bytes 73744 | tf_op jit(solution)/shard_map/reduce_scatter | solution.py:367
  825.7 142.0 %reduce-scatter.15.cloned.1.call-done = f32[24,3072]{1,0:T(8,128)} async-done(((f32[768,3072]{1,0:T(8,128)}), f32[24,3072]{1,0:T(8,128)}) %reduce-scatter.15.cloned.1.call-update) | async-done | bytes 294928 | tf_op jit(solution)/shard_map/reduce_scatter | solution.py:374
  967.7 141.5 %reduce-scatter.17.cloned.1.call-done = f32[96,768]{1,0:T(8,128)} async-done(((f32[3072,768]{1,0:T(8,128)}), f32[96,768]{1,0:T(8,128)}) %reduce-scatter.17.cloned.1.call-update) | async-done | bytes 294928 | tf_op jit(solution)/shard_map/reduce_scatter | solution.py:376
  (265 shorter events, 167.5 us)
Async XLA Ops:
  7.2 69.3 %all-gather.9.cloned.1.call-start = ((), (), s32[]{:S(2)}) async-start(), calls=%async_computation.7 | async-start | bytes 1216512 | tf_op jit(solution)/shard_map/all_gather | solution.py:314
  8.8 115.9 %all-gather.11.cloned.1.call-start = ((), (), s32[]{:S(2)}) async-start(), calls=%async_computation.8 | async-start | bytes 1216512 | tf_op jit(solution)/shard_map/all_gather | solution.py:316
  10.3 170.6 %all-gather.7.cloned.1.call-start = ((), (), s32[]{:S(2)}) async-start(), calls=%async_computation.6 | async-start | bytes 1216512 | tf_op jit(solution)/shard_map/all_gather | solution.py:317
  11.9 225.3 %all-gather.13.cloned.1.call-start = ((), (), s32[]{:S(2)}) async-start(), calls=%async_computation.9 | async-start | bytes 1216512 | tf_op jit(solution)/shard_map/all_gather | solution.py:319
  13.5 289.5 %all-gather.15.cloned.1.call-start = ((), (), s32[]{:S(2)}) async-start(), calls=%async_computation.10 | async-start | bytes 4866048 | tf_op jit(solution)/shard_map/all_gather | solution.py:323
  15.2 352.9 %all-gather.17.cloned.1.call-start = ((), (), s32[]{:S(2)}) async-start(), calls=%async_computation.11 | async-start | bytes 4866048 | tf_op jit(solution)/shard_map/all_gather | solution.py:325
  16.9 648.9 %reduce-scatter.13.cloned.1.call-start = ((), (), s32[]{:S(2)}) async-start(), calls=%async_computation.15 | async-start | bytes 2433024 | tf_op jit(solution)/shard_map/reduce_scatter | solution.py:370
  68.7 112.2 %copy-start.42 = (f32[768]{0:T(1024)}, f32[768]{0:T(1024)S(1)}, u32[]{:S(2)}) copy-start(f32[768]{0:T(1024)S(1)} %convert_element_type.208) | copy-start | bytes 9220
  68.7 112.2 %copy-start.62 = (f32[768]{0:T(1024)}, f32[768]{0:T(1024)S(1)}, u32[]{:S(2)}) copy-start(f32[768]{0:T(1024)S(1)} %convert_element_type.210) | copy-start | bytes 9220
  72.4 164.9 %copy-start.2 = (bf16[1024,768]{0,1:T(8,128)(2,1)}, bf16[1024,768]{0,1:T(8,128)(2,1)S(1)}, u32[]{:S(2)}) copy-start(bf16[1024,768]{0,1:T(8,128)(2,1)S(1)} %copy.45) | copy-start | bytes 4718596
  72.7 108.3 %copy-start.40 = (f32[1024]{0:T(1024)}, f32[1024]{0:T(1024)S(1)}, u32[]{:S(2)}) copy-start(f32[1024]{0:T(1024)S(1)} %broadcast_multiply_fusion.1) | copy-start | bytes 12292
  73.2 107.8 %copy-start.44 = (f32[1024]{0:T(1024)}, f32[1024]{0:T(1024)S(1)}, u32[]{:S(2)}) copy-start(f32[1024]{0:T(1024)S(1)} %fusion.40) | copy-start | bytes 12292
  127.6 70.0 %copy-start.10 = (bf16[1024,768]{0,1:T(8,128)(2,1)}, bf16[1024,768]{0,1:T(8,128)(2,1)S(1)}, u32[]{:S(2)}) copy-start(bf16[1024,768]{0,1:T(8,128)(2,1)S(1)} %convolution_convert_fusion.1) | copy-start | bytes 4718596
  208.3 15.4 %copy-start = (f32[12,512,1024]{2,1,0:T(8,128)S(1)}, f32[12,512,1024]{2,1,0:T(8,128)}, u32[]{:S(2)}) copy-start(f32[12,512,1024]{2,1,0:T(8,128)} %get-tuple-element.94) | copy-start | bytes 75497472
  240.2 62.8 %copy-start.50 = (f32[768]{0:T(1024)S(1)}, f32[768]{0:T(1024)}, u32[]{:S(2)}) copy-start(f32[768]{0:T(1024)} %convert_element_type.229) | copy-start | bytes 9220
  240.2 62.8 %copy-start.57 = (f32[3072]{0:T(1024)S(1)}, f32[3072]{0:T(1024)}, u32[]{:S(2)}) copy-start(f32[3072]{0:T(1024)} %convert_element_type.235) | copy-start | bytes 36868
  240.2 62.8 %copy-start.60 = (f32[768]{0:T(1024)S(1)}, f32[768]{0:T(1024)}, u32[]{:S(2)}) copy-start(f32[768]{0:T(1024)} %convert_element_type.231) | copy-start | bytes 9220
  242.3 161.2 %copy-start.52 = (f32[1024]{0:T(1024)}, f32[1024]{0:T(1024)S(1)}, u32[]{:S(2)}) copy-start(f32[1024]{0:T(1024)S(1)} %fusion.41) | copy-start | bytes 12292
  242.3 125.9 %copy-start.27 = (bf16[1024,768]{1,0:T(8,128)(2,1)S(1)}, bf16[1024,768]{1,0:T(8,128)(2,1)}, u32[]{:S(2)}) copy-start(bf16[1024,768]{1,0:T(8,128)(2,1)} %param.20) | copy-start | bytes 4718596
  414.3 251.5 %reduce-scatter.11.cloned.1.call-start = ((), (), s32[]{:S(2)}) async-start(), calls=%async_computation.14 | async-start | bytes 2433024 | tf_op jit(solution)/shard_map/reduce_scatter | solution.py:368
  485.8 235.5 %reduce-scatter.7.cloned.1.call-start = ((), (), s32[]{:S(2)}) async-start(), calls=%async_computation.12 | async-start | bytes 2433024 | tf_op jit(solution)/shard_map/reduce_scatter | solution.py:365
  550.4 275.3 %reduce-scatter.9.cloned.1.call-start = ((), (), s32[]{:S(2)}) async-start(), calls=%async_computation.13 | async-start | bytes 2433024 | tf_op jit(solution)/shard_map/reduce_scatter | solution.py:367
  568.9 398.7 %reduce-scatter.15.cloned.1.call-start = ((), (), s32[]{:S(2)}) async-start(), calls=%async_computation.16 | async-start | bytes 9732096 | tf_op jit(solution)/shard_map/reduce_scatter | solution.py:374
  579.7 529.4 %reduce-scatter.17.cloned.1.call-start = ((), (), s32[]{:S(2)}) async-start(), calls=%async_computation.17 | async-start | bytes 9732096 | tf_op jit(solution)/shard_map/reduce_scatter | solution.py:376
  (56 other events, 290.0 us)
Sparse Core Ops, SparseCore 0:
  11.4 56.9 all-gather.8
  71.7 52.8 all-gather.10
  128.0 52.9 all-gather.6
  184.2 53.0 all-gather.12
  240.5 62.5 all-gather.14
  306.3 61.8 all-gather.16
  414.4 97.8 reduce-scatter.12
  518.2 98.6 reduce-scatter.10
  622.8 98.5 reduce-scatter.6
  727.1 98.6 reduce-scatter.8
  832.2 135.4 reduce-scatter.14
  974.0 135.1 reduce-scatter.16
where the time goes:
time: 1120 us
  waiting for transfers between devices  608 us (54%)
  matrix products  272 us (24%)
  other arithmetic  101 us (9%)
  blocking collectives  83.2 us (7%)
  local copies, waits for them, and re-layouts  36.4 us (3%)
  between operations  15.1 us (1%)
    reduce_scatter x1, waiting for transfers between devices, shards(): lax.psum_scatter(term_w_up, ('dp', 'fsdp'), scatter_dimension=0, tiled=True)  142 us
    reduce_scatter x1, waiting for transfers between devices, shards(): lax.psum_scatter(term_w_down, ('dp', 'fsdp'), scatter_dimension=0, tiled=...  142 us
    reduce_scatter x1, waiting for transfers between devices, shards(): lax.psum_scatter(term_w_key, ('dp', 'fsdp'), scatter_dimension=0, tiled=T...  104 us
    unnamed x2, blocking collectives  83.2 us
    all_gather x1, waiting for transfers between devices, shards(): lax.all_gather(to_low(w_up), ('dp', 'fsdp'), axis=0, tiled=True)  60.8 us
    dot_general x6, matrix products, matmul(): return jnp.dot(left_arg, right_arg, preferred_element_type=jnp.float32)  59.6 us
    reduce_scatter x1, waiting for transfers between devices, shards(): lax.psum_scatter(term_w_query, ('dp', 'fsdp'), scatter_dimension=0, tiled...  55.5 us
    all_gather x1, waiting for transfers between devices, shards(): lax.all_gather(to_low(w_key), ('dp', 'fsdp'), axis=0, tiled=True)  44 us
  transfers between devices with their start and end apart: 12, of which 9 were waited for; matrix products, arithmetic and copies ran while one was open for 31% of the time, Pallas kernels for 0%

commit v1 on v0

v1 whole, which is shorter than its diff:
```python
import functools

import jax
import jax.numpy as jnp
from jax import lax
from jax.experimental import pallas as pl
from jax.experimental.pallas import tpu as pltpu
from jax.sharding import PartitionSpec as P

HEAD = 64
LANES = 128
QBLOCK = 256
DOC_MAX = 256
NORM_EPSILON = 1e-12
MASK_VALUE = -1e30
AXES = ("dp", "fsdp")
F32 = jnp.float32
BF16 = jnp.bfloat16
VMEM_BYTES = 66_000_000


def mm(a, b, ca, cb):
    return lax.dot_general(a, b, (((ca,), (cb,)), ((), ())), preferred_element_type=F32)


def window(i, length):
    lo = max(0, i * QBLOCK - DOC_MAX)
    hi = min(length, (i + 1) * QBLOCK + DOC_MAX)
    return lo, hi


def norm_parts(v):
    centre = v - jnp.mean(v, axis=-1, keepdims=True)
    spread = jnp.mean(centre * centre, axis=-1, keepdims=True)
    rstd = lax.rsqrt(spread + NORM_EPSILON)
    return centre * rstd, rstd


def fill_bias(segc_ref, segr_ref, bias_ref, length):
    at = 0
    for i in range(length // QBLOCK):
        lo, hi = window(i, length)
        same = segc_ref[lo:hi, :] == segr_ref[:, i * QBLOCK : (i + 1) * QBLOCK]
        bias_ref[at : at + hi - lo, :] = jnp.where(same, 0.0, MASK_VALUE)
        at += hi - lo


def bias_rows(length):
    return sum(window(i, length)[1] - window(i, length)[0] for i in range(length // QBLOCK))


def lane_mask(h):
    lane = lax.broadcasted_iota(jnp.int32, (1, LANES), 1)
    return jnp.where(lax.div(lane, HEAD) == h, 1.0, 0.0)


def attn_fwd_kernel(
    x_ref, wq_ref, wk_ref, wv_ref, vec_ref, bq_ref, bv_ref, segc_ref, segr_ref,
    q_ref, k_ref, v_ref, o_ref, lse_ref, n1_ref, bias_ref, vt_ref,
):
    length = x_ref.shape[0]

    @pl.when(pl.program_id(0) == 0)
    def _():
        xhat, _ = norm_parts(x_ref[...].astype(F32))
        n1_ref[...] = (xhat * vec_ref[0:1, :] + vec_ref[1:2, :]).astype(BF16)
        fill_bias(segc_ref, segr_ref, bias_ref, length)

    n1 = n1_ref[...]
    q_ref[...] = (mm(n1, wq_ref[...], 1, 0) + bq_ref[...]).astype(BF16)
    k_ref[...] = mm(n1, wk_ref[...], 1, 0).astype(BF16)
    v_ref[...] = (mm(n1, wv_ref[...], 1, 0) + bv_ref[...]).astype(BF16)

    def pair(pp, carry):
        cols = pl.ds(pl.multiple_of(pp * LANES, LANES), LANES)
        vt_ref[...] = v_ref[:, cols].T
        at = 0
        for i in range(length // QBLOCK):
            lo, hi = window(i, length)
            rows = slice(i * QBLOCK, (i + 1) * QBLOCK)
            kk = k_ref[lo:hi, cols]
            qq = q_ref[rows, cols].astype(F32) * 0.125
            outs = []
            for h in range(2):
                qm = (qq * lane_mask(h)).astype(BF16)
                s = mm(kk, qm, 1, 1) + bias_ref[at : at + hi - lo, :]
                top = jnp.max(s, axis=0, keepdims=True)
                e = jnp.exp(s - top)
                total = jnp.sum(e, axis=0, keepdims=True)
                pr = (e * (1.0 / total)).astype(BF16)
                outs.append(mm(vt_ref[h * HEAD : (h + 1) * HEAD, lo:hi], pr, 1, 0))
                lse_ref[pp * 2 + h, :, rows] = top + jnp.log(total)
            o_ref[rows, cols] = jnp.concatenate(outs, axis=0).T.astype(BF16)
            at += hi - lo
        return carry

    lax.fori_loop(0, q_ref.shape[1] // LANES, pair, 0)


def full(shape):
    return pl.BlockSpec(shape, lambda *g: (0,) * len(shape), pipeline_mode=pl.Buffered(1))


def attention_forward(x, w_qkv, rows_vec, segc, segr, ):
    length, width = x.shape
    group = 2 * LANES
    steps = width // group
    heads = width // HEAD
    col = pl.BlockSpec((length, group), lambda p: (0, p))
    return pl.pallas_call(
        attn_fwd_kernel,
        grid=(steps,),
        in_specs=[
            full((length, width)),
            pl.BlockSpec((width, group), lambda p: (0, p)),
            pl.BlockSpec((width, group), lambda p: (0, steps + p)),
            pl.BlockSpec((width, group), lambda p: (0, 2 * steps + p)),
            full(rows_vec.shape),
            pl.BlockSpec((1, group), lambda p: (0, p)),
            pl.BlockSpec((1, group), lambda p: (0, p)),
            full((length, 1)),
            full((1, length)),
        ],
        out_specs=[col, col, col, col, pl.BlockSpec((group // HEAD, 1, length), lambda p: (p, 0, 0)),
                   pl.BlockSpec((length, width), lambda p: (0, 0))],
        out_shape=[jax.ShapeDtypeStruct((length, width), BF16)] * 4
        + [jax.ShapeDtypeStruct((heads, 1, length), F32), jax.ShapeDtypeStruct((length, width), BF16)],
        scratch_shapes=[
            pltpu.VMEM((bias_rows(length), QBLOCK), F32),
            pltpu.VMEM((LANES, length), BF16),
        ],
        compiler_params=pltpu.CompilerParams(vmem_limit_bytes=VMEM_BYTES),
        name="attn_fwd",
    )(x, w_qkv, w_qkv, w_qkv, rows_vec, rows_vec[2:3], rows_vec[3:4], segc, segr)


def attn_bwd_kernel(
    q_ref, k_ref, v_ref, g_ref, lse_ref, segc_ref, segr_ref,
    dq_ref, dk_ref, dv_ref, bias_ref, kt_ref, dk_acc, dv_acc,
):
    length = q_ref.shape[0]

    @pl.when(pl.program_id(0) == 0)
    def _():
        fill_bias(segc_ref, segr_ref, bias_ref, length)

    kt_ref[...] = k_ref[...].T
    dk_acc[...] = jnp.zeros_like(dk_acc)
    dv_acc[...] = jnp.zeros_like(dv_acc)
    at = 0
    for i in range(length // QBLOCK):
        lo, hi = window(i, length)
        rows = slice(i * QBLOCK, (i + 1) * QBLOCK)
        kk = k_ref[lo:hi, :]
        vv = v_ref[lo:hi, :]
        qq = q_ref[rows, :].astype(F32) * 0.125
        gg = g_ref[rows, :].astype(F32)
        outs = []
        dk_sum = dv_sum = None
        for h in range(2):
            keep = lane_mask(h)
            qm = (qq * keep).astype(BF16)
            gm = (gg * keep).astype(BF16)
            s = mm(kk, qm, 1, 1) + bias_ref[at : at + hi - lo, :]
            pr = jnp.exp(s - lse_ref[h, :, rows])
            gp = mm(vv, gm, 1, 1)
            centre = jnp.sum(pr * gp, axis=0, keepdims=True)
            gs = (pr * (gp - centre)).astype(BF16)
            dv = mm(pr.astype(BF16), gm, 1, 0)
            dk = mm(gs, qm, 1, 0)
            dk_sum = dk if dk_sum is None else dk_sum + dk
            dv_sum = dv if dv_sum is None else dv_sum + dv
            outs.append(mm(kt_ref[h * HEAD : (h + 1) * HEAD, lo:hi], gs, 1, 0))
        dk_acc[lo:hi, :] += dk_sum
        dv_acc[lo:hi, :] += dv_sum
        dq_ref[rows, :] = (jnp.concatenate(outs, axis=0).T * 0.125).astype(BF16)
        at += hi - lo
    dk_ref[...] = dk_acc[...].astype(BF16)
    dv_ref[...] = dv_acc[...].astype(BF16)


def attention_backward(q, k, v, g, lse, segc, segr):
    length, width = q.shape
    col = pl.BlockSpec((length, LANES), lambda p: (0, p))
    return pl.pallas_call(
        attn_bwd_kernel,
        grid=(width // LANES,),
        in_specs=[col, col, col, col, pl.BlockSpec((2, 1, length), lambda p: (p, 0, 0)),
                  full((length, 1)), full((1, length))],
        out_specs=[col, col, col],
        out_shape=[jax.ShapeDtypeStruct((length, width), BF16)] * 3,
        scratch_shapes=[
            pltpu.VMEM((bias_rows(length), QBLOCK), F32),
            pltpu.VMEM((LANES, length), BF16),
            pltpu.VMEM((length, LANES), F32),
            pltpu.VMEM((length, LANES), F32),
        ],
        compiler_params=pltpu.CompilerParams(vmem_limit_bytes=VMEM_BYTES),
        name="attn_bwd",
    )(q, k, v, g, lse, segc, segr)


LN1_GAIN, LN1_BIAS, B_QUERY, B_VALUE, B_OUT, LN2_GAIN, LN2_BIAS, B_DOWN = range(8)


def ffn_kernel(
    x_ref, mixed_ref, cot_ref, wo_ref, wu_ref, wd_ref, vec_ref, bu_ref,
    out_ref, gh_ref, gm_ref, gwo_ref, gwu_ref, gwd_ref, gvec_ref, gbu_ref,
    h1_ref, n2_ref, n2t_ref, y_ref, gn2_ref,
):
    j = pl.program_id(0)
    last = pl.num_programs(0) - 1

    @pl.when(j == 0)
    def _():
        h1 = x_ref[...].astype(F32) + mm(mixed_ref[...], wo_ref[...], 1, 0) + vec_ref[B_OUT : B_OUT + 1, :]
        h1_ref[...] = h1
        xhat, _ = norm_parts(h1)
        n2 = xhat * vec_ref[LN2_GAIN : LN2_GAIN + 1, :] + vec_ref[LN2_BIAS : LN2_BIAS + 1, :]
        n2 = n2.astype(BF16)
        n2_ref[...] = n2
        n2t_ref[...] = n2.T

    wu = wu_ref[...]
    wd = wd_ref[...]
    cot = cot_ref[...]
    up = mm(n2_ref[...], wu, 1, 0) + bu_ref[...]
    half = 0.5 * (1.0 + lax.erf(up * 0.7071067811865476))
    act = (up * half).astype(BF16)
    slope = half + up * (jnp.exp(-0.5 * up * up) * 0.3989422804014327)
    gu = slope * mm(cot, wd, 1, 1)
    gu = gu.astype(BF16)
    gbu_ref[...] = jnp.sum(gu.astype(F32), axis=0, keepdims=True)
    gwd_ref[...] = mm(act, cot, 0, 0).astype(BF16)
    gwu_ref[...] = mm(n2t_ref[...], gu, 1, 0).astype(BF16)
    y = mm(act, wd, 1, 0)
    gn2 = mm(gu, wu, 1, 1)

    @pl.when(j == 0)
    def _():
        y_ref[...] = y
        gn2_ref[...] = gn2

    @pl.when(j != 0)
    def _():
        y_ref[...] += y
        gn2_ref[...] += gn2

    @pl.when(j == last)
    def _():
        out_ref[...] = (h1_ref[...] + (y_ref[...] + vec_ref[B_DOWN : B_DOWN + 1, :])).astype(BF16)
        xhat, rstd = norm_parts(h1_ref[...])
        gn2_all = gn2_ref[...]
        cot_f = cot_ref[...].astype(F32)
        gvec_ref[...] = jnp.zeros_like(gvec_ref)
        gvec_ref[LN2_GAIN : LN2_GAIN + 1, :] = jnp.sum(gn2_all * xhat, axis=0, keepdims=True)
        gvec_ref[LN2_BIAS : LN2_BIAS + 1, :] = jnp.sum(gn2_all, axis=0, keepdims=True)
        gvec_ref[B_DOWN : B_DOWN + 1, :] = jnp.sum(cot_f, axis=0, keepdims=True)
        gx = gn2_all * vec_ref[LN2_GAIN : LN2_GAIN + 1, :]
        mean_g = jnp.mean(gx, axis=-1, keepdims=True)
        mean_gx = jnp.mean(gx * xhat, axis=-1, keepdims=True)
        gh = cot_f + rstd * (gx - mean_g - xhat * mean_gx)
        gh_ref[...] = gh
        gb = gh.astype(BF16)
        gvec_ref[B_OUT : B_OUT + 1, :] = jnp.sum(gb.astype(F32), axis=0, keepdims=True)
        gwo_ref[...] = mm(mixed_ref[...], gb, 0, 0).astype(BF16)
        gm_ref[...] = mm(gb, wo_ref[...], 1, 1).astype(BF16)


def ffn(x, mixed, cot, wo, wu, wd, vec, bu, block=512):
    length, width = x.shape
    hidden = wu.shape[1]
    const = lambda shape: pl.BlockSpec(shape, lambda j: (0, 0), pipeline_mode=pl.Buffered(1))
    act = (length, width)
    return pl.pallas_call(
        ffn_kernel,
        grid=(hidden // block,),
        in_specs=[
            const(act), const(act), const(act), const(wo.shape),
            pl.BlockSpec((width, block), lambda j: (0, j)),
            pl.BlockSpec((block, width), lambda j: (j, 0)),
            const(vec.shape),
            pl.BlockSpec((1, block), lambda j: (0, j)),
        ],
        out_specs=[
            const(act), const(act), const(act), const(wo.shape),
            pl.BlockSpec((width, block), lambda j: (0, j)),
            pl.BlockSpec((block, width), lambda j: (j, 0)),
            const((8, width)),
            pl.BlockSpec((1, block), lambda j: (0, j)),
        ],
        out_shape=[
            jax.ShapeDtypeStruct(act, BF16),
            jax.ShapeDtypeStruct(act, F32),
            jax.ShapeDtypeStruct(act, BF16),
            jax.ShapeDtypeStruct(wo.shape, BF16),
            jax.ShapeDtypeStruct(wu.shape, BF16),
            jax.ShapeDtypeStruct(wd.shape, BF16),
            jax.ShapeDtypeStruct((8, width), F32),
            jax.ShapeDtypeStruct((1, hidden), F32),
        ],
        scratch_shapes=[
            pltpu.VMEM(act, F32),
            pltpu.VMEM(act, BF16),
            pltpu.VMEM((width, length), BF16),
            pltpu.VMEM(act, F32),
            pltpu.VMEM(act, F32),
        ],
        compiler_params=pltpu.CompilerParams(vmem_limit_bytes=VMEM_BYTES),
        name="ffn",
    )(x, mixed, cot, wo, wu, wd, vec, bu)


def qkv_bwd_kernel(
    x_ref, n1_ref, dq_ref, dk_ref, dv_ref, w_ref, gh_ref, vec_ref,
    gw_ref, gx_ref, gvec_ref, n1t_ref, acc_ref,
):
    j = pl.program_id(0)

    @pl.when(j == 0)
    def _():
        n1t_ref[...] = n1_ref[...].T
        acc_ref[...] = jnp.zeros_like(acc_ref)
        gvec_ref[...] = jnp.zeros_like(gvec_ref)

    def step(d_ref, bias_row):
        d = d_ref[...]
        gw_ref[...] = mm(n1t_ref[...], d, 1, 0).astype(BF16)
        acc_ref[...] += mm(d, w_ref[...], 1, 1)
        if bias_row is not None:
            gvec_ref[bias_row : bias_row + 1, :] = jnp.sum(d.astype(F32), axis=0, keepdims=True)

    @pl.when(j == 0)
    def _():
        step(dq_ref, B_QUERY)

    @pl.when(j == 1)
    def _():
        step(dk_ref, None)

    @pl.when(j == 2)
    def _():
        step(dv_ref, B_VALUE)
        gn1 = acc_ref[...]
        xhat, rstd = norm_parts(x_ref[...].astype(F32))
        gvec_ref[LN1_GAIN : LN1_GAIN + 1, :] = jnp.sum(gn1 * xhat, axis=0, keepdims=True)
        gvec_ref[LN1_BIAS : LN1_BIAS + 1, :] = jnp.sum(gn1, axis=0, keepdims=True)
        gx = gn1 * vec_ref[LN1_GAIN : LN1_GAIN + 1, :]
        mean_g = jnp.mean(gx, axis=-1, keepdims=True)
        mean_gx = jnp.mean(gx * xhat, axis=-1, keepdims=True)
        gx_ref[...] = gh_ref[...] + rstd * (gx - mean_g - xhat * mean_gx)


def qkv_backward(x, n1, dq, dk, dv, w_qkv, gh, vec):
    length, width = x.shape
    act = (length, width)
    const = lambda shape: pl.BlockSpec(shape, lambda j: (0, 0), pipeline_mode=pl.Buffered(1))
    return pl.pallas_call(
        qkv_bwd_kernel,
        grid=(3,),
        in_specs=[const(act)] * 5
        + [pl.BlockSpec((width, width), lambda j: (0, j)), const(act), const(vec.shape)],
        out_specs=[pl.BlockSpec((width, width), lambda j: (0, j)), const(act), const((8, width))],
        out_shape=[
            jax.ShapeDtypeStruct((width, 3 * width), BF16),
            jax.ShapeDtypeStruct(act, F32),
            jax.ShapeDtypeStruct((8, width), F32),
        ],
        scratch_shapes=[pltpu.VMEM((width, length), BF16), pltpu.VMEM(act, F32)],
        compiler_params=pltpu.CompilerParams(vmem_limit_bytes=VMEM_BYTES),
        name="qkv_bwd",
    )(x, n1, dq, dk, dv, w_qkv, gh, vec)


def gather(v):
    return lax.all_gather(v, AXES, axis=0, tiled=True)


def scatter(v):
    return lax.psum_scatter(v, AXES, scatter_dimension=0, tiled=True)


def shards(
    inputs, segment_ids, cotangent, ln1_gain, ln1_bias, w_query, b_query, w_key, w_value, b_value,
    w_out, b_out, ln2_gain, ln2_bias, w_up, b_up, w_down, b_down,
):
    own, width = w_query.shape
    length = inputs.shape[0]
    low = lambda v: v.astype(BF16)
    table = jnp.stack(
        [low(v) for v in (ln1_gain, ln1_bias, b_query, b_value, b_out, ln2_gain, ln2_bias, b_down)], 1
    )
    table = jnp.concatenate([table, low(b_up).reshape(own, -1)], 1)
    table = jnp.pad(table, ((0, 0), (0, LANES - table.shape[1])))
    first = gather(jnp.concatenate([low(w_query), low(w_key), low(w_value), table], 1))
    wo = gather(low(w_out))
    wu = gather(low(w_up))
    wd = gather(low(w_down))
    extra = first[:, 3 * width :].astype(F32)
    vec = extra[:, :8].T
    bu = extra[:, 8 : 8 + w_up.shape[1] // width].reshape(1, -1)
    segc = segment_ids.reshape(length, 1)
    q, k, v, mixed, lse, n1 = attention_forward(inputs, first, vec, segc, segment_ids)
    out, gh, gm, gwo, gwu, gwd, gvec_a, gbu = ffn(inputs, mixed, cotangent, wo, wu, wd, vec, bu)
    dq, dk, dv = attention_backward(q, k, v, gm, lse, segc, segment_ids)
    gw, gx, gvec_b = qkv_backward(inputs, n1, dq, dk, dv, first, gh, vec)
    gtab = jnp.concatenate([(gvec_a + gvec_b).T, gbu.reshape(width, -1)], 1)
    gtab = jnp.pad(gtab, ((0, 0), (0, LANES - gtab.shape[1])))
    s_o = scatter(gwo).astype(F32)
    s_u = scatter(gwu).astype(F32)
    s_d = scatter(gwd).astype(F32)
    s_q = scatter(jnp.concatenate([gw, gtab.astype(BF16)], 1)).astype(F32)
    tab = s_q[:, 3 * width :]
    g1, b1, bq, bv, bo, g2, b2, bd = (tab[:, r] for r in range(8))
    return (
        out, gx, g1, b1, s_q[:, :width], bq, s_q[:, width : 2 * width], s_q[:, 2 * width : 3 * width],
        bv, s_o, bo, g2, b2, s_u, tab[:, 8 : 8 + w_up.shape[1] // width].reshape(-1), s_d, bd,
    )


def solution(mesh):
    row, vec = P(AXES, None), P(AXES)
    weights = (vec, vec, row, vec, row, row, vec, row, vec, vec, vec, row, vec, row, vec)
    return jax.shard_map(
        shards,
        mesh=mesh,
        in_specs=(row, row, row) + weights,
        out_specs=(row, row) + weights,
        check_vma=False,
    )
```

time: 1120 us -> 747 us (0.67)
  matrix products: 272 us -> 0 us
  Pallas kernels: 0 us -> 136 us
  blocking collectives: 83.2 us -> 0 us
  other arithmetic: 101 us -> 25.3 us
  waiting for transfers between devices: 608 us -> 560 us
  local copies, waits for them, and re-layouts: 36.4 us -> 9.86 us
    dot_general x30 -> x0, matrix products: 272 us -> none  [the longest x6 59.6 us: matmul(): return jnp.dot(left_arg, right_arg, preferred_element_type=jnp.float32)]
    reduce_scatter x6 -> x3, waiting for transfers between devices: 443 us -> 257 us  [scatter(): return lax.psum_scatter(v, AXES, scatter_dimension=0, tiled=True)]
    pallas_call x0 -> x4, Pallas kernels: none -> 136 us  [the longest x1 50 us: ffn(): pl.pallas_call(ffn_kernel, grid=(hidden // block,), in_specs=[const(act),...]
    unnamed x12 -> x9, waiting for transfers between devices: 0.2 us -> 99.8 us
    unnamed x2 -> x0, blocking collectives: 83.2 us -> none
    convert_element_type x25 -> x12, other arithmetic: 59.1 us -> 13.8 us  [the longest x7 8.13 us: shards(): low = lambda v: v.astype(BF16)]
    all_gather x6 -> x4, waiting for transfers between devices: 165 us -> 203 us  [gather(): return lax.all_gather(v, AXES, axis=0, tiled=True)]
    reduce_sum x11 -> x0, other arithmetic: 37.2 us -> none  [the longest x2 24.1 us: attend_forward(): row_sum = jnp.sum(raised, axis=-1, keepdims=True)]
  transfers between devices with their start and end apart: 12 -> 8, of which waited for: 9 -> 8; matrix products, arithmetic and copies ran while one was open for 31% -> 3% of each run, Pallas kernels for 0% -> 12%
where the time goes in v1:
time: 747 us; the launch traced here: 746 us
  waiting for transfers between devices  560 us (75%)
  Pallas kernels  136 us (18%)
  other arithmetic  25.3 us (3%)
  between operations  14.3 us (2%)
  local copies, waits for them, and re-layouts  9.86 us (1%)
    reduce_scatter x3, waiting for transfers between devices, scatter(): return lax.psum_scatter(v, AXES, scatter_dimension=0, tiled=True)  257 us
    all_gather x4, waiting for transfers between devices, gather(): return lax.all_gather(v, AXES, axis=0, tiled=True)  203 us
    unnamed x9, waiting for transfers between devices  99.8 us
    pallas_call x1, Pallas kernels, ffn(): pl.pallas_call(ffn_kernel, grid=(hidden // block,), in_specs=[const(act),...  50 us
    pallas_call x1, Pallas kernels, attention_forward(): pl.pallas_call(attn_fwd_kernel, grid=(steps,), in_specs=[full((length, wi...  38.1 us
    pallas_call x1, Pallas kernels, attention_backward(): pl.pallas_call(attn_bwd_kernel, grid=(width // LANES,), in_specs=[col, co...  32.3 us
    pallas_call x1, Pallas kernels, qkv_backward(): pl.pallas_call(qkv_bwd_kernel, grid=(3,), in_specs=[const(act)] * 5 + [pl...  16 us
  transfers between devices with their start and end apart: 8, of which 8 were waited for; matrix products, arithmetic and copies ran while one was open for 3% of the time, Pallas kernels for 12%

profile of v1, /device:TPU:0, one launch (start us, length us, event | category | flops | bytes accessed | tf_op | source)
XLA Modules:
  0.0 746.1 jit_solution(4248670417512726329)
XLA Ops:
  14.0 0.9 convert_element_type.65
  17.6 1.5 convert_element_type.78
  19.2 1.6 convert_element_type.79
  20.9 1.6 convert_element_type.80
  22.6 1.7 copy.66.segc_ref
  24.3 56.8 %all-gather.5.cloned.1.call-done.wq_ref.wk_ref.wv_ref.w_ref = bf16[768,2432]{1,0:T(8,128)(2,1)} async-done(((bf16[24,2432]{1,0:T(8,128)(2,1)}), bf16[768,2432]{1,0:T(8,128)(2,1)}) %all-gather.5.cloned.1.call-update) | async-done | bytes 3735568 | tf_op jit(solution)/shard_map/all_gather | solution.py:376
  81.1 0.9 slice.78
  83.9 38.1 %attn_fwd.1 = (bf16[1024,768]{1,0:T(8,128)(2,1)}, bf16[1024,768]{1,0:T(8,128)(2,1)}, bf16[1024,768]{1,0:T(8,128)(2,1)}, bf16[1024,768]{1,0:T(8,128)(2,1)}, f32[1...) custom-call(bf16[1024,768]{1,0:T(8,128)(2,1)} %x_ref.5, ...), custom_call_target="tpu_custom_call" | custom-call | tf_op jit(solution)/shard_map/attn_fwd/pallas_call | solution.py:110
  122.0 15.1 %all-gather.7.cloned.1.call-done.wo_ref = bf16[768,768]{1,0:T(8,128)(2,1)} async-done(((bf16[24,768]{1,0:T(8,128)(2,1)}), bf16[768,768]{1,0:T(8,128)(2,1)}) %all-gather.7.cloned.1.call-update) | async-done | bytes 1179664 | tf_op jit(solution)/shard_map/all_gather | solution.py:376
  137.2 65.9 %all-gather.9.cloned.1.call-done.wu_ref = bf16[768,3072]{1,0:T(8,128)(2,1)} async-done(((bf16[24,3072]{1,0:T(8,128)(2,1)}), bf16[768,3072]{1,0:T(8,128)(2,1)}) %all-gather.9.cloned.1.call-update) | async-done | bytes 4718608 | tf_op jit(solution)/shard_map/all_gather | solution.py:376
  203.1 65.2 %all-gather.11.cloned.1.call-done.wd_ref = bf16[3072,768]{1,0:T(8,128)(2,1)} async-done(((bf16[96,768]{1,0:T(8,128)(2,1)}), bf16[3072,768]{1,0:T(8,128)(2,1)}) %all-gather.11.cloned.1.call-update) | async-done | bytes 4718608 | tf_op jit(solution)/shard_map/all_gather | solution.py:376
  268.3 50.0 %ffn.1 = (bf16[1024,768]{1,0:T(8,128)(2,1)}, f32[1024,768]{1,0:T(8,128)}, bf16[1024,768]{1,0:T(8,128)(2,1)}, bf16[768,768]{1,0:T(8,128)(2,1)}, bf16[768,3072]{1,...) custom-call(bf16[1024,768]{1,0:T(8,128)(2,1)} %x_ref.5, ...), custom_call_target="tpu_custom_call" | custom-call | tf_op jit(solution)/shard_map/ffn/pallas_call | solution.py:275
  319.6 32.3 %attn_bwd.1 = (bf16[1024,768]{1,0:T(8,128)(2,1)}, bf16[1024,768]{1,0:T(8,128)(2,1)}, bf16[1024,768]{1,0:T(8,128)(2,1)}) custom-call(bf16[1024,768]{1,0:T(8,128)(2,1)} %get-tuple-element.40.q_ref, bf16[1024,768]{1,0:T(8,128)(2,1)} %get-tuple-element.41.k_ref, bf16[1024,768]{1,0:T(8,128)(2,1)} %get-tuple-element.42.v_ref, ...), custom_call_target="tpu_custom_call" | custom-call | tf_op jit(solution)/shard_map/attn_bwd/pallas_call | solution.py:185
  351.9 16.0 %qkv_bwd.1 = (bf16[768,2304]{1,0:T(8,128)(2,1)}, f32[1024,768]{1,0:T(8,128)}, f32[8,768]{1,0:T(8,128)}) custom-call(bf16[1024,768]{1,0:T(8,128)(2,1)} %x_ref.5, bf16[1024,768]{1,0:T(8,128)(2,1)} %get-tuple-element.39.n1_ref, bf16[1024,768]{1,0:T(8,128)(2,1)} %get-tuple-element.45.dq_ref, bf16[1024,768]{1,0:T(8,128)(2,1)} %get-tuple-element.46.dk_ref, ...), custom_call_target="tpu_custom_call" | custom-call | tf_op jit(solution)/shard_map/qkv_bwd/pallas_call | solution.py:358
  368.9 4.2 fusion.1
  374.5 39.3 %reduce-scatter.7.cloned.1.call-done = bf16[24,768]{1,0:T(8,128)(2,1)} async-done(((bf16[768,768]{1,0:T(8,128)(2,1)}), bf16[24,768]{1,0:T(8,128)(2,1)}) %reduce-scatter.7.cloned.1.call-update) | async-done | bytes 36880 | tf_op jit(solution)/shard_map/reduce_scatter | solution.py:380
  413.8 1.4 convert_element_type.82
  415.2 98.3 %reduce-scatter.13.cloned.1.call-done = bf16[24,2432]{1,0:T(8,128)(2,1)} async-done(((bf16[768,2432]{1,0:T(8,128)(2,1)}), bf16[24,2432]{1,0:T(8,128)(2,1)}) %reduce-scatter.13.cloned.1.call-update) | async-done | bytes 116752
  514.9 0.9 convert_element_type.81
  516.6 1.5 fusion.5
  518.1 107.5 %reduce-scatter.11.cloned.1.call-done = bf16[96,768]{1,0:T(8,128)(2,1)} async-done(((bf16[3072,768]{1,0:T(8,128)(2,1)}), bf16[96,768]{1,0:T(8,128)(2,1)}) %reduce-scatter.11.cloned.1.call-update) | async-done | bytes 147472 | tf_op jit(solution)/shard_map/reduce_scatter | solution.py:380
  625.6 1.6 convert_element_type.84
  627.3 110.3 %reduce-scatter.9.cloned.1.call-done = bf16[24,3072]{1,0:T(8,128)(2,1)} async-done(((bf16[768,3072]{1,0:T(8,128)(2,1)}), bf16[24,3072]{1,0:T(8,128)(2,1)}) %reduce-scatter.9.cloned.1.call-update) | async-done | bytes 147472 | tf_op jit(solution)/shard_map/reduce_scatter | solution.py:380
  737.6 1.6 convert_element_type.83
  (58 shorter events, 17.4 us)
Async XLA Ops:
  7.2 74.0 %all-gather.5.cloned.1.call-start = ((), (), s32[]{:S(2)}) async-start(), calls=%async_computation.4 | async-start | bytes 3852288 | tf_op jit(solution)/shard_map/all_gather | solution.py:376
  17.5 119.6 %all-gather.7.cloned.1.call-start = ((), (), s32[]{:S(2)}) async-start(), calls=%async_computation.5 | async-start | bytes 1216512 | tf_op jit(solution)/shard_map/all_gather | solution.py:376
  19.1 184.0 %all-gather.9.cloned.1.call-start = ((), (), s32[]{:S(2)}) async-start(), calls=%async_computation.6 | async-start | bytes 4866048 | tf_op jit(solution)/shard_map/all_gather | solution.py:376
  20.8 247.4 %all-gather.11.cloned.1.call-start = ((), (), s32[]{:S(2)}) async-start(), calls=%async_computation.7 | async-start | bytes 4866048 | tf_op jit(solution)/shard_map/all_gather | solution.py:376
  22.5 391.3 %reduce-scatter.7.cloned.1.call-start = ((), (), s32[]{:S(2)}) async-start(), calls=%async_computation.8 | async-start | bytes 1216512 | tf_op jit(solution)/shard_map/reduce_scatter | solution.py:380
  83.3 0.6 copy-start
  318.2 195.3 %reduce-scatter.13.cloned.1.call-start = ((), (), s32[]{:S(2)}) async-start(), calls=%async_computation.11 | async-start | bytes 3852288
  351.9 16.0 %copy-start.1 = (f32[8,768]{1,0:T(8,128)S(1)}, f32[8,768]{1,0:T(8,128)}, u32[]{:S(2)}) copy-start(f32[8,768]{1,0:T(8,128)} %get-tuple-element.51) | copy-start | bytes 73732
  373.0 252.6 %reduce-scatter.11.cloned.1.call-start = ((), (), s32[]{:S(2)}) async-start(), calls=%async_computation.10 | async-start | bytes 4866048 | tf_op jit(solution)/shard_map/reduce_scatter | solution.py:380
  373.8 363.8 %reduce-scatter.9.cloned.1.call-start = ((), (), s32[]{:S(2)}) async-start(), calls=%async_computation.9 | async-start | bytes 4866048 | tf_op jit(solution)/shard_map/reduce_scatter | solution.py:380
Sparse Core Ops, SparseCore 0:
  17.6 63.4 all-gather.4
  84.5 52.6 all-gather.6
  140.5 62.5 all-gather.8
  206.3 61.8 all-gather.10
  318.4 95.4 reduce-scatter.6
  419.3 94.1 reduce-scatter.12
  519.0 106.5 reduce-scatter.10
  631.1 106.4 reduce-scatter.8
